TPU v7x, 32 devices: a whole 2x2x4 slice. The times are simulated.
32 devices in a mesh: dst: 8 (over z, core), src: 4 (over y, x).
Axes of the slice: x: 2, y: 2, z: 4, core: 2. Of those that a mesh axis runs over, the one named last changes fastest.
Arguments:
- features: bfloat16 [256, 3712], P(('dst', 'src')), may hold values from -6 to 6
- edge_source: int32 [8, 2048], P('dst', 'src'), may hold values from 0 to 255, as said below
- edge_target: int32 [8, 2048], P('dst', 'src'), may hold values from 0 to 255, as said below
- edge_valid: int32 [8, 2048], P('dst', 'src'), may hold values from 0 to 1, as said below
- edge_radial: bfloat16 [8, 2048, 128], P('dst', 'src'), may hold values from -6 to 6
- edge_bias: float32 [8, 8, 2048], P('dst', None, 'src'), may hold values from -10 to 330
- w_radial: bfloat16 [128, 128], replicated, may hold values from -0.5 to 0.5
- w_zero: bfloat16 [896, 896], replicated, may hold values from -0.1875 to 0.1875
- w_one_re: bfloat16 [768, 768], replicated, may hold values from -0.15625 to 0.15625
- w_one_im: bfloat16 [768, 768], replicated, may hold values from -0.15625 to 0.15625
- w_two_re: bfloat16 [640, 640], replicated, may hold values from -0.15625 to 0.15625
- w_two_im: bfloat16 [640, 640], replicated, may hold values from -0.15625 to 0.15625
- att_vector: float32 [128], replicated, may hold values from -3 to 3
- w_out: bfloat16 [7, 128, 128], replicated, may hold values from -0.5 to 0.5
Outputs:
- attended: bfloat16 [256, 3712], P(('dst', 'src'))
Inputs may be any that keep to these rules, and one draw needn't show every extreme that they name: `edge_source`: in row d, column block s (the tile of destination block d and source block s) every entry is an atom a with (a // 8) % 4 == s. `edge_target`: in row d every entry lies in [d * 8 * 4, (d + 1) * 8 * 4); every atom is the target of at least one valid slot. `edge_valid`: about five sixteenths of the slots are valid.
All inputs are finite; a program needn't handle non-finite values.
Results may differ from a plain program's by a relative error of at most 0.0093.
Values may be sent and summed in bfloat16 or wider, within the bound.
A program may use at most 128 MiB of HBM per device.

v0:
```python
import jax
import jax.numpy as jnp
import numpy as np
from jax import lax
from jax.sharding import PartitionSpec as P

HEADS = 8
NCOEF = 29
NEG = -1e30


def merged_2(part, axis, combine):
    gathered = jax.tree.map(lambda a: lax.all_gather(a, axis), part)

    def take(source):
        return jax.tree.map(lambda a: lax.dynamic_index_in_dim(a, source, 0, False), gathered)

    return lax.fori_loop(
        1, lax.axis_size(axis), lambda source, state: combine(state, take(source)), take(0)
    )


def product(left, right):
    return jnp.dot(left, right, preferred_element_type=jnp.float32)


def exact_product(left, right):
    return jnp.dot(left, right, precision=lax.Precision.HIGHEST, preferred_element_type=jnp.float32)


def spread_heads(weights, copies, channels):
    return jnp.tile(jnp.repeat(weights, channels // weights.shape[1], axis=1), (1, copies))


def degree_table():
    return np.array(list(range(7)) + list(range(1, 7)) * 2 + list(range(2, 7)) * 2, dtype=np.int32)


def edge_messages(rows, gain, w_zero, w_one_re, w_one_im, w_two_re, w_two_im, att_vector):
    channels = gain.shape[1]
    count = rows.shape[0]

    def part(low, high):
        return (
            rows[:, low * channels : high * channels].astype(jnp.float32)
            * jnp.tile(gain, (1, high - low))
        ).astype(jnp.bfloat16)

    zero = part(0, 7)
    up_one, uq_one = (part(7, 13), part(13, 19))
    up_two, uq_two = (part(19, 24), part(24, 29))
    out_zero = product(zero, w_zero)
    yp_one = product(up_one, w_one_re) - product(uq_one, w_one_im)
    yq_one = product(up_one, w_one_im) + product(uq_one, w_one_re)
    yp_two = product(up_two, w_two_re) - product(uq_two, w_two_im)
    yq_two = product(up_two, w_two_im) + product(uq_two, w_two_re)
    active = jax.nn.silu(out_zero[:, :channels]) * att_vector[None, :]
    logit = active.reshape(count, HEADS, channels // HEADS).sum(axis=2)
    values = jnp.concatenate([out_zero, yp_one, yq_one, yp_two, yq_two], axis=1)
    return (logit, values)


def shards(
    features,
    edge_source,
    edge_target,
    edge_valid,
    edge_radial,
    edge_bias,
    w_radial,
    w_zero,
    w_one_re,
    w_one_im,
    w_two_re,
    w_two_im,
    att_vector,
    w_out,
):
    channels = w_radial.shape[1]
    own_atoms = features.shape[0]
    block_atoms = own_atoms * lax.axis_size("src")
    gathered = lax.all_gather(features, "dst", axis=0, tiled=True)
    source = edge_source[0]
    target = edge_target[0]
    valid = edge_valid[0] > 0
    slots = source.shape[0]
    local_rows = source // block_atoms * own_atoms + source % own_atoms
    rows = jnp.take(gathered, local_rows, axis=0)
    gain = product(edge_radial[0], w_radial)
    logit, values = edge_messages(
        rows, gain, w_zero, w_one_re, w_one_im, w_two_re, w_two_im, att_vector
    )
    logit = logit + edge_bias[0].T
    local_target = target - lax.axis_index("dst") * block_atoms
    member = (
        lax.broadcasted_iota(jnp.int32, (block_atoms, slots), 0) == local_target[None, :]
    ) & valid[None, :]
    one_hot = member.astype(jnp.float32)
    local_top = jnp.max(jnp.where(member[:, :, None], logit[None, :, :], NEG), axis=1)
    edge_top = exact_product(one_hot.T, local_top)
    shifted = jnp.where(valid[:, None], logit - edge_top, 0.0)
    weights = jnp.where(valid[:, None], jnp.exp(shifted), 0.0)
    weighted = values * spread_heads(weights, NCOEF, channels)
    local_den = exact_product(one_hot, weights)
    local_num = exact_product(one_hot, weighted)

    def combine_states(first, second):
        top = jnp.maximum(first[0], second[0])
        scale_first = jnp.exp(first[0] - top)
        scale_second = jnp.exp(second[0] - top)
        den = first[1] * scale_first + second[1] * scale_second
        num = first[2] * spread_heads(scale_first, NCOEF, channels) + second[2] * spread_heads(
            scale_second, NCOEF, channels
        )
        return (top, den, num)

    merged_top, merged_den, merged_num = merged_2(
        (local_top, local_den, local_num), "src", combine_states
    )
    start = lax.axis_index("src") * own_atoms
    own_den = lax.dynamic_slice_in_dim(merged_den, start, own_atoms, 0)
    own_num = lax.dynamic_slice_in_dim(merged_num, start, own_atoms, 0)
    merged = (own_num / spread_heads(own_den, NCOEF, channels)).astype(jnp.bfloat16)
    selected = w_out[degree_table()]
    projected = jnp.einsum(
        "acx,cxy->acy",
        merged.reshape(own_atoms, NCOEF, channels),
        selected,
        preferred_element_type=jnp.float32,
    )
    return projected.astype(jnp.bfloat16).reshape(own_atoms, NCOEF * channels)


def solution(mesh):
    in_specs = (
        P(("dst", "src"), None),
        P("dst", "src"),
        P("dst", "src"),
        P("dst", "src"),
        P("dst", "src", None),
        P("dst", None, "src"),
        P(),
        P(),
        P(),
        P(),
        P(),
        P(),
        P(),
        P(),
    )
    out_specs = P(("dst", "src"), None)
    return jax.shard_map(shards, mesh=mesh, in_specs=in_specs, out_specs=out_specs, check_vma=False)
```

profile of v0, /device:TPU:0, one launch (start us, length us, event | category | flops | bytes accessed | tf_op | source)
XLA Modules:
  0.0 141.0 jit_solution(15630821081774154500)
XLA Ops:
  6.5 1.2 fusion.13
  7.8 0.7 copy-done.10
  8.8 1.7 %copy.53 = f32[512,896]{1,0:T(8,128)} copy(f32[512,896]{0,1:T(8,128)S(1)} %bitcast.111) | data formatting | bytes 3670016 | tf_op jit(solution)/shard_map/tile | solution.py:46
  10.5 16.4 %all_gather.21 = bf16[64,3712]{1,0:T(8,128)(2,1)S(1)} all-gather(bf16[8,3712]{1,0:T(8,128)(2,1)S(1)} %copy-done.16), channel_id=1, replica_groups=mesh['dst'=8,'src'=4] {'dst'}, dimensions={0}, use_global_device_ids=true | all-gather | bytes 534528 | tf_op jit(solution)/shard_map/all_gather | solution.py:82
  27.0 4.3 %gather_fusion.1 = bf16[512,3712]{1,0:T(8,128)(2,1)} fusion(bf16[64,3712]{1,0:T(8,128)(2,1)S(1)} %all_gather.21, s32[1024]{0:T(1024)S(1)} %pad_clamp_fusion), kind=kCustom, calls=%fused_computation.1 | custom fusion | bytes 7604224 | tf_op jit(solution)/shard_map/jit(_take)/gather | solution.py:88
  31.3 2.7 %broadcast_select_fusion = bf16[512,3712]{1,0:T(8,128)(2,1)S(1)} fusion(bf16[512,3712]{1,0:T(8,128)(2,1)} %gather_fusion.1, pred[512]{0:T(512)(128)(4,1)S(1)} %compare_and_fusion), kind=kLoop, calls=%fused_computation.13 | loop fusion | flops 1900544 | bytes 7602688 | tf_op jit(solution)/shard_map/jit(_take)/select_n | solution.py:88
  34.0 2.5 %constant_dynamic-update-slice_fusion = (f32[512,3712]{1,0:T(8,128)}, f32[512,896]{1,0:T(8,128)S(1)}) fusion(bf16[896,896]{1,0:T(8,128)(2,1)S(1)} %copy-done, f32[512,896]{1,0:T(8,128)S(1)} %copy-done.5, bf16[512,3712]{1,0:T(8,128)(2,1)S(1)} %broadcast_select_fusion), kind=kOutput, calls=%fused_computation.46 | convolution fusion | flops 823459840 | bytes 8028160 | tf_op jit(solution)/shard_map/dot_general | solution.py:24
  37.5 1.4 tile.105
  38.8 1.9 %copy.57 = f32[512,768]{1,0:T(8,128)S(1)} copy(f32[512,768]{0,1:T(8,128)} %bitcast.114) | data formatting | bytes 3145728 | tf_op jit(solution)/shard_map/tile | solution.py:46
  40.7 3.6 %fusion.32 = f32[512,768]{1,0:T(8,128)} fusion(bf16[768,768]{1,0:T(8,128)(2,1)} %param.26, f32[512,768]{1,0:T(8,128)S(1)} %copy.57, bf16[512,3712]{1,0:T(8,128)(2,1)} %copy-done.3), kind=kOutput, calls=%fused_computation.80 | convolution fusion | flops 605159424 | bytes 5111808 | tf_op jit(solution)/shard_map/dot_general | solution.py:24
  44.4 3.1 %fusion.31 = f32[512,768]{1,0:T(8,128)} fusion(bf16[768,768]{1,0:T(8,128)(2,1)S(1)} %copy-done.9, f32[512,768]{1,0:T(8,128)S(1)} %copy.57, bf16[512,3712]{1,0:T(8,128)(2,1)} %copy-done.3), kind=kOutput, calls=%fused_computation.79 | convolution fusion | flops 605159424 | bytes 5111808 | tf_op jit(solution)/shard_map/dot_general | solution.py:24
  47.4 1.2 tile.107
  48.7 2.8 %copy.60 = f32[512,640]{1,0:T(8,128)} copy(f32[512,640]{0,1:T(8,128)} %bitcast.115) | data formatting | bytes 2621440 | tf_op jit(solution)/shard_map/tile | solution.py:46
  51.5 3.7 %fusion.30 = f32[512,640]{1,0:T(8,128)} fusion(bf16[640,640]{1,0:T(8,128)(2,1)} %param.28, f32[512,640]{1,0:T(8,128)} %copy.60, bf16[512,3712]{1,0:T(8,128)(2,1)} %copy-done.3), kind=kOutput, calls=%fused_computation.78 | convolution fusion | flops 420413440 | bytes 4096000 | tf_op jit(solution)/shard_map/dot_general | solution.py:24
  55.2 2.9 %fusion.29 = f32[512,640]{1,0:T(8,128)} fusion(bf16[640,640]{1,0:T(8,128)(2,1)S(1)} %copy-done.13, f32[512,640]{1,0:T(8,128)S(1)} %copy-done.1, bf16[512,3712]{1,0:T(8,128)(2,1)} %copy-done.3), kind=kOutput, calls=%fused_computation.77 | convolution fusion | flops 420413440 | bytes 4096000 | tf_op jit(solution)/shard_map/dot_general | solution.py:24
  58.1 4.0 %tile.110 = f32[512,29,128]{0,2,1:T(8,128)} broadcast(f32[512,128]{0,1:T(8,128)S(1)} %bitcast.117), dimensions={0,2} | broadcast | bytes 7864320 | tf_op jit(solution)/shard_map/tile | solution.py:32
  62.2 8.8 %copy.62 = f32[512,3712]{1,0:T(8,128)} copy(f32[512,3712]{0,1:T(8,128)} %bitcast.110) | data formatting | bytes 15204352 | tf_op jit(solution)/shard_map/tile | solution.py:32
  71.0 4.1 %subtract_dynamic-update-slice_fusion = f32[512,3712]{1,0:T(8,128)} fusion(f32[512,3712]{1,0:T(8,128)} %get-tuple-element.202, f32[512,768]{1,0:T(8,128)} %fusion.32, bf16[768,768]{1,0:T(8,128)(2,1)} %param.27, f32[512,768]{1,0:T(8,128)S(1)} %copy.57, bf16[512,3712]{1,0:T(8,128)(2,1)} %copy-done.3), kind=kOutput, calls=%fused_computation.16 | convolution fusion | flops 605552640 | bytes 6684672 | tf_op jit(solution)/shard_map/dot_general | solution.py:24
  75.2 3.5 %add_dynamic-update-slice_fusion = f32[512,3712]{1,0:T(8,128)} fusion(f32[512,3712]{1,0:T(8,128)} %subtract_dynamic-update-slice_fusion, f32[512,768]{1,0:T(8,128)S(1)} %copy-done.6, bf16[768,768]{1,0:T(8,128)(2,1)} %param.26, f32[512,768]{1,0:T(8,128)S(1)} %copy.57, bf16[512,3712]{1,0:T(8,128)(2,1)S(1)} %copy-done.4), kind=kOutput, calls=%fused_computation.15 | convolution fusion | flops 605552640 | bytes 6684672 | tf_op jit(solution)/shard_map/dot_general | solution.py:24
  78.7 1.9 %fusion.6 = f32[512,3712]{1,0:T(8,128)} fusion(f32[512,3712]{1,0:T(8,128)} %add_dynamic-update-slice_fusion, f32[512,640]{1,0:T(8,128)S(1)} %copy-done.8, bf16[640,640]{1,0:T(8,128)(2,1)S(1)} %copy-done.14, f32[512,640]{1,0:T(8,128)S(1)} %copy-done.2, bf16[512,3712]{1,0:T(8,128)(2,1)S(1)} %copy-done.4), kind=kOutput, calls=%fused_computation.22 | convolution fusion | flops 420741120 | bytes 5406720 | tf_op jit(solution)/shard_map/dot_general | solution.py:24
  80.6 1.9 %fusion.5 = f32[512,3712]{1,0:T(8,128)} fusion(f32[512,3712]{1,0:T(8,128)} %fusion.6, f32[512,640]{1,0:T(8,128)S(1)} %copy-done.7, bf16[640,640]{1,0:T(8,128)(2,1)S(1)} %copy-done.15, f32[512,640]{1,0:T(8,128)S(1)} %copy-done.2, bf16[512,3712]{1,0:T(8,128)(2,1)S(1)} %copy-done.4), kind=kOutput, calls=%fused_computation.20 | convolution fusion | flops 420741120 | bytes 5406720 | tf_op jit(solution)/shard_map/dot_general | solution.py:24
  82.6 7.2 %fusion.3 = f32[32,3712]{1,0:T(8,128)} fusion(f32[512,3712]{1,0:T(8,128)} %fusion.5, f32[512,3712]{1,0:T(8,128)S(1)} %bitcast.109, s32[512]{0:T(512)S(1)} %bitcast.121, pred[512]{0:T(512)(128)(4,1)S(1)} %compare_reduce_fusion), kind=kOutput, calls=%fused_computation.11 | convolution fusion | flops 731742208 | bytes 15682048 | tf_op jit(solution)/shard_map/dot_general | solution.py:28
  89.9 1.6 %gather_fusion = bf16[29,128,128]{2,1,0:T(8,128)(2,1)} fusion(bf16[7,128,128]{2,1,0:T(8,128)(2,1)S(1)} %copy-done.12, s32[1024]{0:T(1024)S(1)} %pad_clamp_fusion.1), kind=kCustom, calls=%fused_computation | custom fusion | bytes 1900660 | tf_op jit(solution)/shard_map/gather | solution.py:124
  91.5 8.2 %all-gather.3 = f32[4,32,8]{1,2,0:T(8,128)S(1)} all-gather(f32[1,32,8]{1,2,0:T(8,128)S(1)} %copy.55), channel_id=2, replica_groups=mesh['dst'=8,'src'=4] {'src'}, dimensions={0}, use_global_device_ids=true | all-gather | bytes 5120 | tf_op jit(solution)/shard_map/all_gather | solution.py:13
  99.8 8.4 %all-gather.4 = f32[4,32,8]{1,2,0:T(8,128)S(1)} all-gather(f32[1,32,8]{1,2,0:T(8,128)S(1)} %convolution_bitcast_fusion), channel_id=3, replica_groups=mesh['dst'=8,'src'=4] {'src'}, dimensions={0}, use_global_device_ids=true | all-gather | bytes 5120 | tf_op jit(solution)/shard_map/all_gather | solution.py:13
  108.2 16.4 %all-gather.7.cloned.1.call-done = f32[128,3712]{1,0:T(8,128)} async-done(((f32[32,3712]{1,0:T(8,128)}), f32[128,3712]{1,0:T(8,128)}) %all-gather.7.cloned.1.call-update) | async-done | bytes 1900560 | tf_op jit(solution)/shard_map/all_gather | solution.py:13
  124.7 1.1 slice.44
  125.7 5.9 %while.19 = (s32[]{:T(128)}, f32[32,8]{0,1:T(8,128)S(1)}, f32[32,8]{0,1:T(8,128)S(1)}, f32[32,3712]{1,0:T(8,128)S(1)}, f32[4,32,8]{1,2,0:T(8,128)S(1)}, /*index=...) while((s32[]{:T(128)}, f32[32,8]{0,1:T(8,128)S(1)}, ...), condition=%wide.region_3.4_spmd, body=%wide.region_2.3_spmd.sunk | while | flops 357893 | bytes 3467415 | solution.py:18
  126.0 1.7 %fusion.50 = f32[32,3712]{1,0:T(8,128)S(1)} fusion(f32[4,8,29,128]{3,2,1,0:T(8,128)S(1)} %bitcast.106, f32[32,3712]{1,0:T(8,128)S(1)} %get-tuple-element.268, f32[4,8,29,128]{3,2,1,0:T(8,128)S(1)} %bitcast.107, f32[4,32,3712]{2,1,0:T(8,128)} %get-tuple-element.281, s32[]{:T(128)S(6)} %select_n.137), kind=kLoop, calls=%fused_computation.3.clone.1 | loop fusion | flops 356352 | bytes 2375684 | tf_op jit(solution)/shard_map/while/body/eval_jaxpr/add | solution.py:112
  128.0 1.7 %fusion.50 = f32[32,3712]{1,0:T(8,128)S(1)} fusion(f32[4,8,29,128]{3,2,1,0:T(8,128)S(1)} %bitcast.106, f32[32,3712]{1,0:T(8,128)S(1)} %get-tuple-element.268, f32[4,8,29,128]{3,2,1,0:T(8,128)S(1)} %bitcast.107, f32[4,32,3712]{2,1,0:T(8,128)} %get-tuple-element.281, s32[]{:T(128)S(6)} %select_n.137), kind=kLoop, calls=%fused_computation.3.clone.1 | loop fusion | flops 356352 | bytes 2375684 | tf_op jit(solution)/shard_map/while/body/eval_jaxpr/add | solution.py:112
  130.0 1.7 %fusion.50 = f32[32,3712]{1,0:T(8,128)S(1)} fusion(f32[4,8,29,128]{3,2,1,0:T(8,128)S(1)} %bitcast.106, f32[32,3712]{1,0:T(8,128)S(1)} %get-tuple-element.268, f32[4,8,29,128]{3,2,1,0:T(8,128)S(1)} %bitcast.107, f32[4,32,3712]{2,1,0:T(8,128)} %get-tuple-element.281, s32[]{:T(128)S(6)} %select_n.137), kind=kLoop, calls=%fused_computation.3.clone.1 | loop fusion | flops 356352 | bytes 2375684 | tf_op jit(solution)/shard_map/while/body/eval_jaxpr/add | solution.py:112
  132.0 2.2 %fusion.7 = bf16[8,3712]{1,0:T(8,128)(2,1)} fusion(bf16[29,128,128]{2,1,0:T(8,128)(2,1)} %gather_fusion, f32[32,3712]{1,0:T(8,128)S(1)} %get-tuple-element.182, s32[]{:T(128)S(6)} %select_n.99, f32[8,128]{1,0:T(8,128)S(1)} %tile.112), kind=kOutput, calls=%fused_computation.26 | convolution fusion | flops 7691264 | bytes 1132548 | tf_op jit(solution)/shard_map/acx,cxy->acy/dot_general | solution.py:125
  (96 shorter events, 2.5 us)
Async XLA Ops:
  6.5 27.4 %copy-start = (bf16[896,896]{1,0:T(8,128)(2,1)S(1)}, bf16[896,896]{1,0:T(8,128)(2,1)}, u32[]{:S(2)}) copy-start(bf16[896,896]{1,0:T(8,128)(2,1)} %param.25) | copy-start | bytes 4816900
  6.5 118.1 %all-gather.7.cloned.1.call-start = ((), (), s32[]{:S(2)}) async-start(), calls=%async_computation | async-start | bytes 2375680 | tf_op jit(solution)/shard_map/all_gather | solution.py:13
  7.8 0.7 copy-start.10
  8.7 1.7 %copy-start.16 = (bf16[8,3712]{1,0:T(8,128)(2,1)S(1)}, bf16[8,3712]{1,0:T(8,128)(2,1)}, u32[]{:S(2)}) copy-start(bf16[8,3712]{1,0:T(8,128)(2,1)} %param.18) | copy-start | bytes 178180
  8.8 18.1 %copy-start.18 = (s32[1,512]{1,0:T(1,128)S(1)}, s32[1,512]{1,0:T(1,128)}, u32[]{:S(2)}) copy-start(s32[1,512]{1,0:T(1,128)} %param.19) | copy-start | bytes 6148
  31.3 2.7 %copy-start.5 = (f32[512,896]{1,0:T(8,128)S(1)}, f32[512,896]{1,0:T(8,128)}, u32[]{:S(2)}) copy-start(f32[512,896]{1,0:T(8,128)} %copy.53) | copy-start | bytes 5505028
  34.0 2.6 %copy-start.3 = (bf16[512,3712]{1,0:T(8,128)(2,1)}, bf16[512,3712]{1,0:T(8,128)(2,1)S(1)}, u32[]{:S(2)}) copy-start(bf16[512,3712]{1,0:T(8,128)(2,1)S(1)} %broadcast_select_fusion) | copy-start | bytes 11403268
  34.0 2.6 %copy-start.21 = (f32[128]{0:T(128)S(1)}, f32[128]{0:T(128)}, u32[]{:S(2)}) copy-start(f32[128]{0:T(128)} %param.30) | copy-start | bytes 1540
  34.0 2.8 %copy-start.19 = (s32[1,512]{1,0:T(1,128)S(1)}, s32[1,512]{1,0:T(1,128)}, u32[]{:S(2)}) copy-start(s32[1,512]{1,0:T(1,128)} %param.21) | copy-start | bytes 6148
  34.0 2.8 %copy-start.17 = (f32[1,8,512]{2,1,0:T(8,128)S(1)}, f32[1,8,512]{2,1,0:T(8,128)}, u32[]{:S(2)}) copy-start(f32[1,8,512]{2,1,0:T(8,128)} %param.23) | copy-start | bytes 49156
  34.0 2.9 %copy-start.20 = (s32[1,512]{1,0:T(1,128)S(1)}, s32[1,512]{1,0:T(1,128)}, u32[]{:S(2)}) copy-start(s32[1,512]{1,0:T(1,128)} %param.20) | copy-start | bytes 6148
  36.5 1.0 copy-start.11
  40.7 3.7 %copy-start.9 = (bf16[768,768]{1,0:T(8,128)(2,1)S(1)}, bf16[768,768]{1,0:T(8,128)(2,1)}, u32[]{:S(2)}) copy-start(bf16[768,768]{1,0:T(8,128)(2,1)} %param.27) | copy-start | bytes 3538948
  51.4 3.7 %copy-start.1 = (f32[512,640]{1,0:T(8,128)S(1)}, f32[512,640]{1,0:T(8,128)}, u32[]{:S(2)}) copy-start(f32[512,640]{1,0:T(8,128)} %copy.60) | copy-start | bytes 3932164
  51.4 3.7 %copy-start.13 = (bf16[640,640]{1,0:T(8,128)(2,1)S(1)}, bf16[640,640]{1,0:T(8,128)(2,1)}, u32[]{:S(2)}) copy-start(bf16[640,640]{1,0:T(8,128)(2,1)} %param.29) | copy-start | bytes 2457604
  71.0 4.2 %copy-start.4 = (bf16[512,3712]{1,0:T(8,128)(2,1)S(1)}, bf16[512,3712]{1,0:T(8,128)(2,1)}, u32[]{:S(2)}) copy-start(bf16[512,3712]{1,0:T(8,128)(2,1)} %copy-done.3) | copy-start | bytes 11403268
  71.0 4.2 %copy-start.6 = (f32[512,768]{1,0:T(8,128)S(1)}, f32[512,768]{1,0:T(8,128)}, u32[]{:S(2)}) copy-start(f32[512,768]{1,0:T(8,128)} %fusion.31) | copy-start | bytes 4718596
  71.0 7.7 %copy-start.8 = (f32[512,640]{1,0:T(8,128)S(1)}, f32[512,640]{1,0:T(8,128)}, u32[]{:S(2)}) copy-start(f32[512,640]{1,0:T(8,128)} %fusion.30) | copy-start | bytes 3932164
  75.1 3.5 %copy-start.2 = (f32[512,640]{1,0:T(8,128)S(1)}, f32[512,640]{1,0:T(8,128)}, u32[]{:S(2)}) copy-start(f32[512,640]{1,0:T(8,128)} %copy.60) | copy-start | bytes 3932164
  75.2 3.5 %copy-start.14 = (bf16[640,640]{1,0:T(8,128)(2,1)S(1)}, bf16[640,640]{1,0:T(8,128)(2,1)}, u32[]{:S(2)}) copy-start(bf16[640,640]{1,0:T(8,128)(2,1)} %param.29) | copy-start | bytes 2457604
  75.2 5.4 %copy-start.15 = (bf16[640,640]{1,0:T(8,128)(2,1)S(1)}, bf16[640,640]{1,0:T(8,128)(2,1)}, u32[]{:S(2)}) copy-start(bf16[640,640]{1,0:T(8,128)(2,1)} %param.28) | copy-start | bytes 2457604
  75.2 7.4 %slice-start = ((s8[7602176]{0:T(1024)(128)(4,1)}), s8[4194304]{0:T(1024)(128)(4,1)S(1)}, s32[]{:S(2)}) async-start(s8[7602176]{0:T(1024)(128)(4,1)} %bitcast.108), calls=%async_computation.1 | async-start | bytes 8388608
  78.7 1.9 %copy-start.7 = (f32[512,640]{1,0:T(8,128)S(1)}, f32[512,640]{1,0:T(8,128)}, u32[]{:S(2)}) copy-start(f32[512,640]{1,0:T(8,128)} %fusion.29) | copy-start | bytes 3932164
  78.7 3.8 %slice-start.1 = ((s8[7602176]{0:T(1024)(128)(4,1)}), s8[3407872]{0:T(1024)(128)(4,1)S(1)}, s32[]{:S(2)}) async-start(s8[7602176]{0:T(1024)(128)(4,1)} %bitcast.108), calls=%async_computation.2 | async-start | bytes 6815744
  82.5 7.3 %copy-start.22 = (s32[29]{0:T(128)S(1)}, s32[29]{0:T(128)}, u32[]{:S(2)}) copy-start(s32[29]{0:T(128)} %constant.134) | copy-start | bytes 352
  82.5 7.3 %copy-start.12 = (bf16[7,128,128]{2,1,0:T(8,128)(2,1)S(1)}, bf16[7,128,128]{2,1,0:T(8,128)(2,1)}, u32[]{:S(2)}) copy-start(bf16[7,128,128]{2,1,0:T(8,128)(2,1)} %param.31) | copy-start | bytes 688132
Sparse Core Ops, SparseCore 0:
  89.9 34.7 all-gather.6
where the time goes:
time: 142 us; the launch traced here: 141 us
  matrix products  38.3 us (27%)
  blocking collectives  33 us (23%)
  local copies, waits for them, and re-layouts  31.2 us (22%)
  waiting for transfers between devices  16.5 us (12%)
  between operations  13.7 us (10%)
  other arithmetic  8.12 us (6%)
    dot_general x10, matrix products, product(): return jnp.dot(left, right, preferred_element_type=jnp.float32)  28.6 us
    all_gather x2, blocking collectives, merged_2(): gathered = jax.tree.map(lambda a: lax.all_gather(a, axis), part)  16.6 us
    all_gather x1, waiting for transfers between devices, merged_2(): gathered = jax.tree.map(lambda a: lax.all_gather(a, axis), part)  16.4 us
    all_gather x1, blocking collectives, shards(): gathered = lax.all_gather(features, 'dst', axis=0, tiled=True)  16.4 us
    another operation x15, local copies, waits for them, and re-layouts, spread_heads(): jnp.tile(jnp.repeat(weights, channels // weights.shape[1], axis=1), (1, c...  13.6 us
    another operation x6, local copies, waits for them, and re-layouts, part(): jnp.tile(gain, (1, high - low))  9.16 us
    dot_general x3, matrix products, exact_product(): jnp.dot(left, right, precision=lax.Precision.HIGHEST, preferred_element_t...  7.55 us
    add x3, other arithmetic, combine_states(): first[2] * spread_heads(scale_first, NCOEF, channels)  5.02 us
  transfers between devices with their start and end apart: 1, of which 1 were waited for; matrix products, arithmetic and copies ran while one was open for 1% of the time, Pallas kernels for 0%

commit v1 on v0

--- a/solution.py
+++ b/solution.py
@@ -7,6 +7,14 @@
 HEADS = 8
 NCOEF = 29
 NEG = -1e30
+
+
+def test_signs(x_in):
+    last = jnp.stack(tuple((x_in for _ in range(lax.axis_size("dst")))))
+    x_new = jnp.concatenate(
+        lax.all_to_all(last, axis_name="dst", split_axis=0, concat_axis=0), axis=0
+    )
+    return x_new
 
 
 def merged_2(part, axis, combine):
@@ -79,7 +87,7 @@
     channels = w_radial.shape[1]
     own_atoms = features.shape[0]
     block_atoms = own_atoms * lax.axis_size("src")
-    gathered = lax.all_gather(features, "dst", axis=0, tiled=True)
+    gathered = test_signs(features)
     source = edge_source[0]
     target = edge_target[0]
     valid = edge_valid[0] > 0

time: 142 us -> 133 us (0.937)
  blocking collectives: 33 us -> 16.6 us
  starting transfers between devices: 0.01 us -> 6.39 us
  matrix products: 38.3 us -> 34 us
  local copies, waits for them, and re-layouts: 31.2 us -> 34.8 us
  other arithmetic: 8.12 us -> 9.76 us
    all_gather x1 -> x0, blocking collectives: 16.4 us -> none  [shards(): gathered = lax.all_gather(features, 'dst', axis=0, tiled=True)]
    all_to_all x0 -> x1, starting transfers between devices: none -> 6.35 us  [test_signs(): lax.all_to_all(last, axis_name='dst', split_axis=0, concat_axis=0)]
    dot_general x10, matrix products: 28.6 us -> 24.2 us  [product(): return jnp.dot(left, right, preferred_element_type=jnp.float32)]
    another operation x6, local copies, waits for them, and re-layouts: 9.16 us -> 11.2 us  [part(): jnp.tile(gain, (1, high - low))]
    another operation x0 -> x1, local copies, waits for them, and re-layouts: none -> 1.76 us  [test_signs(): last = jnp.stack(tuple((x_in for _ in range(lax.axis_size('dst')))))]
  transfers between devices with their start and end apart: 1 -> 2, of which waited for: 1 -> 2; matrix products, arithmetic and copies ran while one was open for 1% -> 11% of each run, Pallas kernels for 0% -> 0%
where the time goes in v1:
time: 133 us; the launch traced here: 132 us
  local copies, waits for them, and re-layouts  34.8 us (26%)
  matrix products  34 us (26%)
  waiting for transfers between devices  16.8 us (13%)
  blocking collectives  16.6 us (12%)
  between operations  13.8 us (10%)
  other arithmetic  9.76 us (7%)
  starting transfers between devices  6.39 us (5%)
    dot_general x10, matrix products, product(): return jnp.dot(left, right, preferred_element_type=jnp.float32)  24.2 us
    all_gather x2, blocking collectives, merged_2(): gathered = jax.tree.map(lambda a: lax.all_gather(a, axis), part)  16.6 us
    all_gather x1, waiting for transfers between devices, merged_2(): gathered = jax.tree.map(lambda a: lax.all_gather(a, axis), part)  15.6 us
    another operation x15, local copies, waits for them, and re-layouts, spread_heads(): jnp.tile(jnp.repeat(weights, channels // weights.shape[1], axis=1), (1, c...  13.6 us
    another operation x6, local copies, waits for them, and re-layouts, part(): jnp.tile(gain, (1, high - low))  11.2 us
    dot_general x3, matrix products, exact_product(): jnp.dot(left, right, precision=lax.Precision.HIGHEST, preferred_element_t...  7.55 us
    all_to_all x1, starting transfers between devices, test_signs(): lax.all_to_all(last, axis_name='dst', split_axis=0, concat_axis=0)  6.35 us
    add x3, other arithmetic, combine_states(): first[2] * spread_heads(scale_first, NCOEF, channels)  5.02 us
  transfers between devices with their start and end apart: 2, of which 2 were waited for; matrix products, arithmetic and copies ran while one was open for 11% of the time, Pallas kernels for 0%

profile of v1, /device:TPU:0, one launch (start us, length us, event | category | flops | bytes accessed | tf_op | source)
XLA Modules:
  0.0 132.3 jit_solution(14200272617324551065)
XLA Ops:
  6.5 1.8 %stack.2 = bf16[8,8,3712]{2,1,0:T(8,128)(2,1)} broadcast(bf16[8,3712]{1,0:T(8,128)(2,1)} %param.18), dimensions={1,2} | broadcast | bytes 534528 | tf_op jit(solution)/shard_map/stack | solution.py:13
  8.3 6.4 %all-to-all-start = ((bf16[8,8,3712]{2,1,0:T(8,128)(2,1)}), bf16[8,8,3712]{2,1,0:T(8,128)(2,1)S(1)}, u32[]{:S(2)}, u32[]{:S(2)}) async-start(bf16[8,8,3712]{2,1,0:T(8,128)(2,1)} %stack.2), calls=%async_computation | async-start | bytes 950272 | tf_op jit(solution)/shard_map/all_to_all | solution.py:15
  16.4 1.5 %tile.103 = f32[512,7,128]{0,2,1:T(8,128)} broadcast(f32[512,128]{0,1:T(8,128)S(1)} %fusion.13), dimensions={0,2} | broadcast | bytes 2097152 | tf_op jit(solution)/shard_map/tile | solution.py:54
  17.9 2.8 %copy.53 = f32[512,896]{1,0:T(8,128)} copy(f32[512,896]{0,1:T(8,128)} %bitcast.113) | data formatting | bytes 3670016 | tf_op jit(solution)/shard_map/tile | solution.py:54
  20.7 1.4 %tile.105 = f32[512,6,128]{0,2,1:T(8,128)} broadcast(f32[512,128]{0,1:T(8,128)S(1)} %fusion.13), dimensions={0,2} | broadcast | bytes 1835008 | tf_op jit(solution)/shard_map/tile | solution.py:54
  22.1 3.1 %copy.57 = f32[512,768]{1,0:T(8,128)} copy(f32[512,768]{0,1:T(8,128)} %bitcast.116) | data formatting | bytes 3145728 | tf_op jit(solution)/shard_map/tile | solution.py:54
  25.1 1.1 tile.107
  26.3 1.5 %copy.60 = f32[512,640]{1,0:T(8,128)} copy(f32[512,640]{0,1:T(8,128)S(1)} %bitcast.117) | data formatting | bytes 2621440 | tf_op jit(solution)/shard_map/tile | solution.py:54
  27.8 1.1 all-to-all-done
  28.9 4.3 %gather_fusion.1 = bf16[512,3712]{1,0:T(8,128)(2,1)} fusion(bf16[64,3712]{1,0:T(8,128)(2,1)S(1)} %bitcast.107, s32[1024]{0:T(1024)S(1)} %pad_clamp_fusion), kind=kCustom, calls=%fused_computation.1 | custom fusion | bytes 7604224 | tf_op jit(solution)/shard_map/jit(_take)/gather | solution.py:96
  33.2 2.7 %broadcast_select_fusion = bf16[512,3712]{1,0:T(8,128)(2,1)S(1)} fusion(bf16[512,3712]{1,0:T(8,128)(2,1)} %gather_fusion.1, pred[512]{0:T(512)(128)(4,1)S(1)} %compare_and_fusion), kind=kLoop, calls=%fused_computation.13 | loop fusion | flops 1900544 | bytes 7602688 | tf_op jit(solution)/shard_map/jit(_take)/select_n | solution.py:96
  36.0 2.5 %constant_dynamic-update-slice_fusion = (f32[512,3712]{1,0:T(8,128)}, f32[512,896]{1,0:T(8,128)S(1)}) fusion(bf16[896,896]{1,0:T(8,128)(2,1)S(1)} %copy-done, f32[512,896]{1,0:T(8,128)S(1)} %copy-done.7, bf16[512,3712]{1,0:T(8,128)(2,1)S(1)} %broadcast_select_fusion), kind=kOutput, calls=%fused_computation.46 | convolution fusion | flops 823459840 | bytes 8028160 | tf_op jit(solution)/shard_map/dot_general | solution.py:32
  40.8 3.7 %fusion.32 = f32[512,768]{1,0:T(8,128)} fusion(bf16[768,768]{1,0:T(8,128)(2,1)} %param.26, f32[512,768]{1,0:T(8,128)S(1)} %copy-done.1, bf16[512,3712]{1,0:T(8,128)(2,1)} %copy-done.4), kind=kOutput, calls=%fused_computation.80 | convolution fusion | flops 605159424 | bytes 5111808 | tf_op jit(solution)/shard_map/dot_general | solution.py:32
  44.5 1.9 %fusion.31 = f32[512,768]{1,0:T(8,128)} fusion(bf16[768,768]{1,0:T(8,128)(2,1)S(1)} %copy-done.11, f32[512,768]{1,0:T(8,128)S(1)} %copy-done.1, bf16[512,3712]{1,0:T(8,128)(2,1)S(1)} %copy-done.5), kind=kOutput, calls=%fused_computation.79 | convolution fusion | flops 605159424 | bytes 5111808 | tf_op jit(solution)/shard_map/dot_general | solution.py:32
  46.5 1.9 %fusion.30 = f32[512,640]{1,0:T(8,128)} fusion(bf16[640,640]{1,0:T(8,128)(2,1)S(1)} %copy-done.16, f32[512,640]{1,0:T(8,128)S(1)} %copy-done.2, bf16[512,3712]{1,0:T(8,128)(2,1)S(1)} %copy-done.5), kind=kOutput, calls=%fused_computation.78 | convolution fusion | flops 420413440 | bytes 4096000 | tf_op jit(solution)/shard_map/dot_general | solution.py:32
  48.3 1.8 %fusion.29 = f32[512,640]{1,0:T(8,128)} fusion(bf16[640,640]{1,0:T(8,128)(2,1)S(1)} %copy-done.14, f32[512,640]{1,0:T(8,128)S(1)} %copy-done.2, bf16[512,3712]{1,0:T(8,128)(2,1)S(1)} %copy-done.5), kind=kOutput, calls=%fused_computation.77 | convolution fusion | flops 420413440 | bytes 4096000 | tf_op jit(solution)/shard_map/dot_general | solution.py:32
  50.2 4.0 %tile.110 = f32[512,29,128]{0,2,1:T(8,128)} broadcast(f32[512,128]{0,1:T(8,128)S(1)} %bitcast.119), dimensions={0,2} | broadcast | bytes 7864320 | tf_op jit(solution)/shard_map/tile | solution.py:40
  54.2 8.8 %copy.62 = f32[512,3712]{1,0:T(8,128)} copy(f32[512,3712]{0,1:T(8,128)} %bitcast.112) | data formatting | bytes 15204352 | tf_op jit(solution)/shard_map/tile | solution.py:40
  63.1 4.2 %subtract_dynamic-update-slice_fusion = f32[512,3712]{1,0:T(8,128)} fusion(f32[512,3712]{1,0:T(8,128)} %get-tuple-element.202, f32[512,768]{1,0:T(8,128)} %fusion.32, bf16[768,768]{1,0:T(8,128)(2,1)} %param.27, f32[512,768]{1,0:T(8,128)S(1)} %copy-done.1, bf16[512,3712]{1,0:T(8,128)(2,1)} %copy-done.4), kind=kOutput, calls=%fused_computation.16 | convolution fusion | flops 605552640 | bytes 6684672 | tf_op jit(solution)/shard_map/dot_general | solution.py:32
  67.3 3.4 %add_dynamic-update-slice_fusion = f32[512,3712]{1,0:T(8,128)} fusion(f32[512,3712]{1,0:T(8,128)} %subtract_dynamic-update-slice_fusion, f32[512,768]{1,0:T(8,128)S(1)} %copy-done.8, bf16[768,768]{1,0:T(8,128)(2,1)} %param.26, f32[512,768]{1,0:T(8,128)S(1)} %copy-done.1, bf16[512,3712]{1,0:T(8,128)(2,1)S(1)} %copy-done.6), kind=kOutput, calls=%fused_computation.15 | convolution fusion | flops 605552640 | bytes 6684672 | tf_op jit(solution)/shard_map/dot_general | solution.py:32
  70.7 1.9 %fusion.6 = f32[512,3712]{1,0:T(8,128)} fusion(f32[512,3712]{1,0:T(8,128)} %add_dynamic-update-slice_fusion, f32[512,640]{1,0:T(8,128)S(1)} %copy-done.10, bf16[640,640]{1,0:T(8,128)(2,1)S(1)} %copy-done.15, f32[512,640]{1,0:T(8,128)S(1)} %copy-done.3, bf16[512,3712]{1,0:T(8,128)(2,1)S(1)} %copy-done.6), kind=kOutput, calls=%fused_computation.22 | convolution fusion | flops 420741120 | bytes 5406720 | tf_op jit(solution)/shard_map/dot_general | solution.py:32
  72.6 1.9 %fusion.5 = f32[512,3712]{1,0:T(8,128)} fusion(f32[512,3712]{1,0:T(8,128)} %fusion.6, f32[512,640]{1,0:T(8,128)S(1)} %copy-done.9, bf16[640,640]{1,0:T(8,128)(2,1)S(1)} %copy-done.17, f32[512,640]{1,0:T(8,128)S(1)} %copy-done.3, bf16[512,3712]{1,0:T(8,128)(2,1)S(1)} %copy-done.6), kind=kOutput, calls=%fused_computation.20 | convolution fusion | flops 420741120 | bytes 5406720 | tf_op jit(solution)/shard_map/dot_general | solution.py:32
  74.6 7.2 %fusion.3 = f32[32,3712]{1,0:T(8,128)} fusion(f32[512,3712]{1,0:T(8,128)} %fusion.5, f32[512,3712]{1,0:T(8,128)S(1)} %bitcast.111, s32[512]{0:T(512)S(1)} %bitcast.123, pred[512]{0:T(512)(128)(4,1)S(1)} %compare_reduce_fusion), kind=kOutput, calls=%fused_computation.11 | convolution fusion | flops 731742208 | bytes 15682048 | tf_op jit(solution)/shard_map/dot_general | solution.py:36
  81.8 1.6 %gather_fusion = bf16[29,128,128]{2,1,0:T(8,128)(2,1)} fusion(bf16[7,128,128]{2,1,0:T(8,128)(2,1)S(1)} %copy-done.13, s32[1024]{0:T(1024)S(1)} %pad_clamp_fusion.1), kind=kCustom, calls=%fused_computation | custom fusion | bytes 1900660 | tf_op jit(solution)/shard_map/gather | solution.py:132
  83.5 8.2 %all-gather.3 = f32[4,32,8]{1,2,0:T(8,128)S(1)} all-gather(f32[1,32,8]{1,2,0:T(8,128)S(1)} %copy.55), channel_id=2, replica_groups=mesh['dst'=8,'src'=4] {'src'}, dimensions={0}, use_global_device_ids=true | all-gather | bytes 5120 | tf_op jit(solution)/shard_map/all_gather | solution.py:21
  91.8 8.5 %all-gather.4 = f32[4,32,8]{1,2,0:T(8,128)S(1)} all-gather(f32[1,32,8]{1,2,0:T(8,128)S(1)} %convolution_bitcast_fusion), channel_id=3, replica_groups=mesh['dst'=8,'src'=4] {'src'}, dimensions={0}, use_global_device_ids=true | all-gather | bytes 5120 | tf_op jit(solution)/shard_map/all_gather | solution.py:21
  100.3 15.6 %all-gather.7.cloned.1.call-done = f32[128,3712]{1,0:T(8,128)} async-done(((f32[32,3712]{1,0:T(8,128)}), f32[128,3712]{1,0:T(8,128)}) %all-gather.7.cloned.1.call-update) | async-done | bytes 1900560 | tf_op jit(solution)/shard_map/all_gather | solution.py:21
  117.0 5.9 %while.19 = (s32[]{:T(128)}, f32[32,8]{0,1:T(8,128)S(1)}, f32[32,8]{0,1:T(8,128)S(1)}, f32[32,3712]{1,0:T(8,128)S(1)}, f32[4,32,8]{1,2,0:T(8,128)S(1)}, /*index=...) while((s32[]{:T(128)}, f32[32,8]{0,1:T(8,128)S(1)}, ...), condition=%wide.region_3.4_spmd, body=%wide.region_2.3_spmd.sunk | while | flops 357893 | bytes 3467415 | solution.py:26
  117.3 1.7 %fusion.50 = f32[32,3712]{1,0:T(8,128)S(1)} fusion(f32[4,8,29,128]{3,2,1,0:T(8,128)S(1)} %bitcast.108, f32[32,3712]{1,0:T(8,128)S(1)} %get-tuple-element.268, f32[4,8,29,128]{3,2,1,0:T(8,128)S(1)} %bitcast.109, f32[4,32,3712]{2,1,0:T(8,128)} %get-tuple-element.281, s32[]{:T(128)S(6)} %select_n.137), kind=kLoop, calls=%fused_computation.3.clone.1 | loop fusion | flops 356352 | bytes 2375684 | tf_op jit(solution)/shard_map/while/body/eval_jaxpr/add | solution.py:120
  119.3 1.7 %fusion.50 = f32[32,3712]{1,0:T(8,128)S(1)} fusion(f32[4,8,29,128]{3,2,1,0:T(8,128)S(1)} %bitcast.108, f32[32,3712]{1,0:T(8,128)S(1)} %get-tuple-element.268, f32[4,8,29,128]{3,2,1,0:T(8,128)S(1)} %bitcast.109, f32[4,32,3712]{2,1,0:T(8,128)} %get-tuple-element.281, s32[]{:T(128)S(6)} %select_n.137), kind=kLoop, calls=%fused_computation.3.clone.1 | loop fusion | flops 356352 | bytes 2375684 | tf_op jit(solution)/shard_map/while/body/eval_jaxpr/add | solution.py:120
  121.2 1.7 %fusion.50 = f32[32,3712]{1,0:T(8,128)S(1)} fusion(f32[4,8,29,128]{3,2,1,0:T(8,128)S(1)} %bitcast.108, f32[32,3712]{1,0:T(8,128)S(1)} %get-tuple-element.268, f32[4,8,29,128]{3,2,1,0:T(8,128)S(1)} %bitcast.109, f32[4,32,3712]{2,1,0:T(8,128)} %get-tuple-element.281, s32[]{:T(128)S(6)} %select_n.137), kind=kLoop, calls=%fused_computation.3.clone.1 | loop fusion | flops 356352 | bytes 2375684 | tf_op jit(solution)/shard_map/while/body/eval_jaxpr/add | solution.py:120
  123.2 2.2 %fusion.7 = bf16[8,3712]{1,0:T(8,128)(2,1)} fusion(bf16[29,128,128]{2,1,0:T(8,128)(2,1)} %gather_fusion, f32[32,3712]{1,0:T(8,128)S(1)} %get-tuple-element.182, s32[]{:T(128)S(6)} %select_n.99, f32[8,128]{1,0:T(8,128)S(1)} %tile.112), kind=kOutput, calls=%fused_computation.26 | convolution fusion | flops 7691264 | bytes 1132548 | tf_op jit(solution)/shard_map/acx,cxy->acy/dot_general | solution.py:133
  (102 shorter events, 6.5 us)
Async XLA Ops:
  6.5 29.4 %copy-start = (bf16[896,896]{1,0:T(8,128)(2,1)S(1)}, bf16[896,896]{1,0:T(8,128)(2,1)}, u32[]{:S(2)}) copy-start(bf16[896,896]{1,0:T(8,128)(2,1)} %param.25) | copy-start | bytes 4816900
  6.5 8.9 %copy-start.18 = (bf16[1,512,128]{2,1,0:T(8,128)(2,1)S(1)}, bf16[1,512,128]{2,1,0:T(8,128)(2,1)}, u32[]{:S(2)}) copy-start(bf16[1,512,128]{2,1,0:T(8,128)(2,1)} %param.22) | copy-start | bytes 393220
  8.3 20.6 %all-to-all-start = ((bf16[8,8,3712]{2,1,0:T(8,128)(2,1)}), bf16[8,8,3712]{2,1,0:T(8,128)(2,1)S(1)}, u32[]{:S(2)}, u32[]{:S(2)}) async-start(bf16[8,8,3712]{2,1,0:T(8,128)(2,1)} %stack.2), calls=%async_computation | async-start | bytes 950272 | tf_op jit(solution)/shard_map/all_to_all | solution.py:15
  14.7 101.3 %all-gather.7.cloned.1.call-start = ((), (), s32[]{:S(2)}) async-start(), calls=%async_computation.1 | async-start | bytes 2375680 | tf_op jit(solution)/shard_map/all_gather | solution.py:21
  16.4 4.3 %copy-start.12 = (f32[512,128]{0,1:T(8,128)}, f32[512,128]{0,1:T(8,128)S(1)}, u32[]{:S(2)}) copy-start(f32[512,128]{0,1:T(8,128)S(1)} %fusion.13) | copy-start | bytes 786436
  26.2 1.5 %copy-start.21 = (s32[1,512]{1,0:T(1,128)S(1)}, s32[1,512]{1,0:T(1,128)}, u32[]{:S(2)}) copy-start(s32[1,512]{1,0:T(1,128)} %param.21) | copy-start | bytes 6148
  26.2 1.5 %copy-start.20 = (s32[1,512]{1,0:T(1,128)S(1)}, s32[1,512]{1,0:T(1,128)}, u32[]{:S(2)}) copy-start(s32[1,512]{1,0:T(1,128)} %param.19) | copy-start | bytes 6148
  26.2 1.5 %copy-start.22 = (s32[1,512]{1,0:T(1,128)S(1)}, s32[1,512]{1,0:T(1,128)}, u32[]{:S(2)}) copy-start(s32[1,512]{1,0:T(1,128)} %param.20) | copy-start | bytes 6148
  33.2 2.7 %copy-start.7 = (f32[512,896]{1,0:T(8,128)S(1)}, f32[512,896]{1,0:T(8,128)}, u32[]{:S(2)}) copy-start(f32[512,896]{1,0:T(8,128)} %copy.53) | copy-start | bytes 5505028
  35.9 2.6 %copy-start.4 = (bf16[512,3712]{1,0:T(8,128)(2,1)}, bf16[512,3712]{1,0:T(8,128)(2,1)S(1)}, u32[]{:S(2)}) copy-start(bf16[512,3712]{1,0:T(8,128)(2,1)S(1)} %broadcast_select_fusion) | copy-start | bytes 11403268
  35.9 2.6 %copy-start.23 = (f32[128]{0:T(128)S(1)}, f32[128]{0:T(128)}, u32[]{:S(2)}) copy-start(f32[128]{0:T(128)} %param.30) | copy-start | bytes 1540
  35.9 4.5 %copy-start.19 = (f32[1,8,512]{2,1,0:T(8,128)S(1)}, f32[1,8,512]{2,1,0:T(8,128)}, u32[]{:S(2)}) copy-start(f32[1,8,512]{2,1,0:T(8,128)} %param.23) | copy-start | bytes 49156
  35.9 4.8 %copy-start.1 = (f32[512,768]{1,0:T(8,128)S(1)}, f32[512,768]{1,0:T(8,128)}, u32[]{:S(2)}) copy-start(f32[512,768]{1,0:T(8,128)} %copy.57) | copy-start | bytes 4718596
  40.8 3.7 %copy-start.5 = (bf16[512,3712]{1,0:T(8,128)(2,1)S(1)}, bf16[512,3712]{1,0:T(8,128)(2,1)}, u32[]{:S(2)}) copy-start(bf16[512,3712]{1,0:T(8,128)(2,1)} %copy-done.4) | copy-start | bytes 11403268
  40.8 3.7 %copy-start.11 = (bf16[768,768]{1,0:T(8,128)(2,1)S(1)}, bf16[768,768]{1,0:T(8,128)(2,1)}, u32[]{:S(2)}) copy-start(bf16[768,768]{1,0:T(8,128)(2,1)} %param.27) | copy-start | bytes 3538948
  44.5 2.0 %copy-start.2 = (f32[512,640]{1,0:T(8,128)S(1)}, f32[512,640]{1,0:T(8,128)}, u32[]{:S(2)}) copy-start(f32[512,640]{1,0:T(8,128)} %copy.60) | copy-start | bytes 3932164
  44.5 1.9 %copy-start.16 = (bf16[640,640]{1,0:T(8,128)(2,1)S(1)}, bf16[640,640]{1,0:T(8,128)(2,1)}, u32[]{:S(2)}) copy-start(bf16[640,640]{1,0:T(8,128)(2,1)} %param.28) | copy-start | bytes 2457604
  46.5 1.9 %copy-start.14 = (bf16[640,640]{1,0:T(8,128)(2,1)S(1)}, bf16[640,640]{1,0:T(8,128)(2,1)}, u32[]{:S(2)}) copy-start(bf16[640,640]{1,0:T(8,128)(2,1)} %param.29) | copy-start | bytes 2457604
  63.0 4.2 %copy-start.6 = (bf16[512,3712]{1,0:T(8,128)(2,1)S(1)}, bf16[512,3712]{1,0:T(8,128)(2,1)}, u32[]{:S(2)}) copy-start(bf16[512,3712]{1,0:T(8,128)(2,1)} %copy-done.4) | copy-start | bytes 11403268
  63.0 4.2 %copy-start.8 = (f32[512,768]{1,0:T(8,128)S(1)}, f32[512,768]{1,0:T(8,128)}, u32[]{:S(2)}) copy-start(f32[512,768]{1,0:T(8,128)} %fusion.31) | copy-start | bytes 4718596
  63.1 7.7 %copy-start.10 = (f32[512,640]{1,0:T(8,128)S(1)}, f32[512,640]{1,0:T(8,128)}, u32[]{:S(2)}) copy-start(f32[512,640]{1,0:T(8,128)} %fusion.30) | copy-start | bytes 3932164
  67.3 3.5 %copy-start.3 = (f32[512,640]{1,0:T(8,128)S(1)}, f32[512,640]{1,0:T(8,128)}, u32[]{:S(2)}) copy-start(f32[512,640]{1,0:T(8,128)} %copy.60) | copy-start | bytes 3932164
  67.3 3.5 %copy-start.15 = (bf16[640,640]{1,0:T(8,128)(2,1)S(1)}, bf16[640,640]{1,0:T(8,128)(2,1)}, u32[]{:S(2)}) copy-start(bf16[640,640]{1,0:T(8,128)(2,1)} %param.29) | copy-start | bytes 2457604
  67.3 5.4 %copy-start.17 = (bf16[640,640]{1,0:T(8,128)(2,1)S(1)}, bf16[640,640]{1,0:T(8,128)(2,1)}, u32[]{:S(2)}) copy-start(bf16[640,640]{1,0:T(8,128)(2,1)} %param.28) | copy-start | bytes 2457604
  67.3 7.2 %slice-start = ((s8[7602176]{0:T(1024)(128)(4,1)}), s8[4194304]{0:T(1024)(128)(4,1)S(1)}, s32[]{:S(2)}) async-start(s8[7602176]{0:T(1024)(128)(4,1)} %bitcast.110), calls=%async_computation.2 | async-start | bytes 8388608
  70.7 1.9 %copy-start.9 = (f32[512,640]{1,0:T(8,128)S(1)}, f32[512,640]{1,0:T(8,128)}, u32[]{:S(2)}) copy-start(f32[512,640]{1,0:T(8,128)} %fusion.29) | copy-start | bytes 3932164
  70.7 3.8 %slice-start.1 = ((s8[7602176]{0:T(1024)(128)(4,1)}), s8[3407872]{0:T(1024)(128)(4,1)S(1)}, s32[]{:S(2)}) async-start(s8[7602176]{0:T(1024)(128)(4,1)} %bitcast.110), calls=%async_computation.3 | async-start | bytes 6815744
  74.5 7.3 %copy-start.24 = (s32[29]{0:T(128)S(1)}, s32[29]{0:T(128)}, u32[]{:S(2)}) copy-start(s32[29]{0:T(128)} %constant.134) | copy-start | bytes 352
  74.5 7.3 %copy-start.13 = (bf16[7,128,128]{2,1,0:T(8,128)(2,1)S(1)}, bf16[7,128,128]{2,1,0:T(8,128)(2,1)}, u32[]{:S(2)}) copy-start(bf16[7,128,128]{2,1,0:T(8,128)(2,1)} %param.31) | copy-start | bytes 688132
Sparse Core Ops, SparseCore 0:
  81.9 33.9 all-gather.6
